TPU v7x, 128 devices: a whole 4x4x4 slice. The times are simulated.
128 devices in a mesh: batch: 32 (over y, z, core), mp: 4 (over x).
Axes of the slice: x: 4, y: 4, z: 4, core: 2. Of those that a mesh axis runs over, the one named last changes fastest.
Arguments:
- init_state: float32 [16384, 256], P(('batch', 'mp')), may hold values from -6 to 6
- brownian: bfloat16 [32, 16384, 256], P(None, ('batch', 'mp')), may hold values from -6 to 6
- step_size: float32 [16384], P(('batch', 'mp')), may hold values from 0.02 to 0.1
- lengths: int32 [16384], P(('batch', 'mp')), may hold values from 1 to 32, as said below
- obs_steps: int32 [16384, 8], P(('batch', 'mp')), may hold values from 1 to 32, as said below
- observed: bfloat16 [16384, 8, 128], P(('batch', 'mp')), may hold values from -6 to 6
- w_in: bfloat16 [256, 1024], P(None, 'mp'), may hold values from -0.375 to 0.375
- b_in: bfloat16 [1024], P('mp'), may hold values from -3 to 3
- w_out: bfloat16 [1024, 256], P('mp'), may hold values from -0.1875 to 0.1875
- b_out: float32 [256], replicated, may hold values from -4 to 4
- decoder: bfloat16 [256, 128], replicated, may hold values from -0.375 to 0.375
- prior_rate: float32 [256], replicated, may hold values from 0.1 to 2
- diffusion: float32 [256], replicated, may hold values from 0.7 to 1.4
Outputs:
- elbo_series: float32 [16384], P(('batch', 'mp'))
- scores: float32 [2], replicated
- grad_w_in: float32 [256, 1024], P(None, 'mp')
- grad_b_in: float32 [1024], P('mp')
- grad_w_out: float32 [1024, 256], P('mp')
- grad_b_out: float32 [256], replicated
- grad_decoder: float32 [256, 128], replicated
- grad_init: float32 [16384, 256], P(('batch', 'mp'))
Inputs may be any that keep to these rules, and one draw needn't show every extreme that they name: `lengths`: some series has 32 live steps in every draw. obs_steps[i, j] is at most lengths[i].
All inputs are finite; a program needn't handle non-finite values.
Results may differ from a plain program's by a relative error of at most 0.0019.
Values may be sent and summed in bfloat16 or wider, within the bound.
A program may use at most 64 MiB of HBM per device.

v0:
```python
import jax
import jax.numpy as jnp
from jax import lax
from jax.experimental import pallas as pl
from jax.experimental.pallas import tpu as pltpu
from jax.sharding import PartitionSpec as P

F32 = jnp.float32
BF16 = jnp.bfloat16
NT = (((1,), (1,)), ((), ()))


def dot(a, b):
    return jnp.dot(a, b, preferred_element_type=F32)


def dot_nt(a, b):
    return lax.dot_general(a, b, NT, preferred_element_type=F32)


def fold(value):
    return value.reshape(-1, 8, value.shape[1]).sum(axis=0)


def core_kernel(
    init_ref,
    noise_ref,
    step_ref,
    length_ref,
    obs_ref,
    seen_ref,
    w_in_ref,
    b_in_ref,
    w_out_ref,
    b_out_ref,
    dec_ref,
    rate_ref,
    diff_ref,
    elbo_ref,
    grads_ref,
    cot_ref,
    x_ref,
    xt_ref,
    ut_ref,
    act_ref,
    pre_ref,
    scaled_ref,
    pick_ref,
    obs_wide_ref,
    dt_ref,
    root_ref,
    len_ref,
    state_ref,
    kl_ref,
    sum_b_in_ref,
    sum_b_out_ref,
    miss_ref,
    target_ref,
):
    rows, width = init_ref.shape
    steps = noise_ref.shape[0]
    seen_count = obs_ref.shape[0]
    seen_width = dec_ref.shape[1]
    chunks = w_in_ref.shape[0]

    def column(row):
        return jnp.broadcast_to(row, (rows, rows)).T

    dt_ref[...] = column(step_ref[...])
    root_ref[...] = jnp.sqrt(dt_ref[...])
    len_ref[...] = column(length_ref[...])
    for j in range(seen_count):
        obs_wide_ref[j] = column(obs_ref[j : j + 1, :])
    target_ref[...] = seen_ref[...].astype(F32).reshape(target_ref.shape)
    pick_ref[...] = jnp.zeros_like(pick_ref)
    kl_ref[...] = jnp.zeros_like(kl_ref)
    sum_b_in_ref[...] = jnp.zeros_like(sum_b_in_ref)
    sum_b_out_ref[...] = jnp.zeros_like(sum_b_out_ref)
    state_ref[...] = init_ref[...]
    x_ref[0] = init_ref[...].astype(BF16)

    def both(value):
        return jnp.concatenate([value] * (width // rows), axis=1)

    def forward(k, carry):
        x = x_ref[k]
        drift = jnp.broadcast_to(b_out_ref[...], (rows, width))
        for n in range(chunks):
            act = jnp.tanh(dot(x, w_in_ref[n]) + b_in_ref[n, :1, :]).astype(BF16)
            act_ref[n, pl.ds(k * rows, rows), :] = act
            drift = drift + dot(act, w_out_ref[n])
        state = state_ref[...]
        inv = 1.0 / diff_ref[...]
        live = k < len_ref[...]
        factor = both(jnp.where(live, dt_ref[...], 0.0))
        root = both(jnp.where(live, root_ref[...], 0.0))
        residual = (drift + rate_ref[...] * state) * inv
        kl_ref[...] += factor * residual * residual
        scaled_ref[k] = residual * inv
        following = state + (
            factor * drift + diff_ref[...] * root * noise_ref[k].astype(F32)
        )
        state_ref[...] = following
        rounded = following.astype(BF16)
        x_ref[k + 1] = rounded
        xt_ref[:, pl.ds(pl.multiple_of(k * rows, rows), rows)] = x.T
        seen = dot(rounded, dec_ref[...])
        for j in range(seen_count):
            pick_ref[j] = jnp.where(obs_wide_ref[j] == k + 1, seen, pick_ref[j])
        return carry

    lax.fori_loop(0, steps, forward, 0)

    square = jnp.zeros((rows, seen_width), F32)
    for j in range(seen_count):
        misfit = pick_ref[j] - target_ref[pl.ds(j, rows, stride=seen_count), :]
        square = square + misfit * misfit
        pick_ref[j] = misfit.astype(BF16).astype(F32)
    loglik = -0.5 * jnp.sum(square.T, axis=0, keepdims=True)
    kl_half = kl_ref[:, :rows]
    for part in range(1, width // rows):
        kl_half = kl_half + kl_ref[:, part * rows : (part + 1) * rows]
    kl_row = 0.5 * jnp.sum(kl_half.T, axis=0, keepdims=True)
    divisor = (width * length_ref[...] + seen_width * seen_count).astype(F32)
    elbo_ref[...] = (loglik - kl_row) / divisor

    cot_ref[...] = jnp.zeros_like(cot_ref)

    def backward(index, carry):
        k = steps - 1 - index
        total = jnp.zeros((rows, seen_width), F32)
        for j in range(seen_count):
            total = total + jnp.where(obs_wide_ref[j] == k + 1, pick_ref[j], 0.0)
        high = total.astype(BF16)
        low = (total - high.astype(F32)).astype(BF16)
        miss_ref[pl.ds(k * rows, rows), :seen_width] = high
        miss_ref[pl.ds(k * rows, rows), seen_width:] = low
        obs_back = dot_nt(high, dec_ref[...]) + dot_nt(low, dec_ref[...])
        cot = cot_ref[...] + obs_back
        scaled = scaled_ref[k]
        factor = both(jnp.where(k < len_ref[...], dt_ref[...], 0.0))
        update = factor * (cot + scaled)
        rounded = update.astype(BF16)
        ut_ref[:, pl.ds(pl.multiple_of(k * rows, rows), rows)] = rounded.T
        sum_b_out_ref[...] += fold(update)
        cot = cot + factor * rate_ref[...] * scaled
        for n in range(chunks):
            act = act_ref[n, pl.ds(k * rows, rows), :].astype(F32)
            pre = dot_nt(rounded, w_out_ref[n]) * (1.0 - act * act)
            sum_b_in_ref[n] += fold(pre)
            pre_round = pre.astype(BF16)
            pre_ref[n, pl.ds(k * rows, rows), :] = pre_round
            cot = cot + dot_nt(pre_round, w_in_ref[n])
        cot_ref[...] = cot
        return carry

    lax.fori_loop(0, steps, backward, 0)

    def gradients(n, carry):
        grads_ref[n, :width, :] = dot(xt_ref[...], pre_ref[n])
        grads_ref[n, width : 2 * width, :] = dot(ut_ref[...], act_ref[n]).T
        return carry

    lax.fori_loop(0, chunks, gradients, 0)

    dec_grad = jnp.zeros((width, 2 * seen_width), F32)
    dec_grad = dec_grad + dot(xt_ref[:, rows:], miss_ref[: (steps - 1) * rows, :])
    last = lax.dot_general(
        x_ref[steps],
        miss_ref[(steps - 1) * rows :, :],
        (((0,), (0,)), ((), ())),
        preferred_element_type=F32,
    )
    dec_grad = dec_grad + last
    dec_grad = dec_grad[:, :seen_width] + dec_grad[:, seen_width:]
    lanes = width // seen_width
    share = width // chunks
    tail = 2 * width
    line = tail + share // lanes
    for n in range(chunks):
        pieces = [
            dec_grad[n * share + m * share // lanes : n * share + (m + 1) * share // lanes, :]
            for m in range(lanes)
        ]
        grads_ref[n, tail:line, :] = jnp.concatenate(pieces, axis=1)
        grads_ref[n, line:, :] = jnp.zeros((grads_ref.shape[1] - line, width), F32)
        grads_ref[n, line : line + 1, :] = jnp.sum(sum_b_in_ref[n], axis=0, keepdims=True)
        grads_ref[n, line + 1 : line + 2, :] = jnp.sum(
            sum_b_out_ref[...], axis=0, keepdims=True
        )
        grads_ref[n, line + 2 : line + 3, :rows] = loglik
        grads_ref[n, line + 2 : line + 3, rows : 2 * rows] = kl_row


def core(grad_rows, init, noise, step, length, obs, seen, w_in, b_in, w_out, b_out, dec, rate, diff):
    rows, width = init.shape
    steps = noise.shape[0]
    seen_count, seen_width = seen.shape[1], dec.shape[1]
    chunks = w_in.shape[0]
    vmem = pl.BlockSpec(memory_space=pltpu.VMEM)
    out = [
        jax.ShapeDtypeStruct((1, rows), F32),
        jax.ShapeDtypeStruct((chunks, grad_rows, width), F32),
        jax.ShapeDtypeStruct((rows, width), F32),
    ]
    resident = (6, 7, 8)
    operands = (init, noise, step, length, obs, seen, w_in, b_in, w_out, b_out, dec, rate, diff)
    loaded = [i for i in range(len(operands)) if i not in resident]
    specs = [
        vmem if i in resident else pl.BlockSpec(memory_space=pltpu.HBM)
        for i in range(len(operands))
    ]

    def body(*refs):
        refs = list(refs)
        sems = refs.pop()
        spaces = [refs.pop() for _ in loaded][::-1]
        copies = []
        for at, (i, space) in enumerate(zip(loaded, spaces)):
            copy = pltpu.make_async_copy(refs[i], space, sems.at[at])
            copy.start()
            copies.append(copy)
            refs[i] = space
        for copy in copies:
            copy.wait()
        core_kernel(*refs)

    scratch = [
        pltpu.VMEM((steps + 1, rows, width), BF16),
        pltpu.VMEM((width, steps * rows), BF16),
        pltpu.VMEM((width, steps * rows), BF16),
        pltpu.VMEM((chunks, steps * rows, width), BF16),
        pltpu.VMEM((chunks, steps * rows, width), BF16),
        pltpu.VMEM((steps, rows, width), F32),
        pltpu.VMEM((seen_count, rows, seen_width), F32),
        pltpu.VMEM((seen_count, rows, rows), jnp.int32),
        pltpu.VMEM((rows, rows), F32),
        pltpu.VMEM((rows, rows), F32),
        pltpu.VMEM((rows, rows), jnp.int32),
        pltpu.VMEM((rows, width), F32),
        pltpu.VMEM((rows, width), F32),
        pltpu.VMEM((chunks, 8, width), F32),
        pltpu.VMEM((8, width), F32),
        pltpu.VMEM((steps * rows, 2 * seen_width), BF16),
        pltpu.VMEM((rows * seen_count, seen_width), F32),
    ]
    scratch += [pltpu.VMEM(operands[i].shape, operands[i].dtype) for i in loaded]
    scratch += [pltpu.SemaphoreType.DMA((len(loaded),))]
    return pl.pallas_call(
        body,
        out_shape=out,
        in_specs=specs,
        out_specs=[vmem] * 3,
        scratch_shapes=scratch,
        compiler_params=pltpu.CompilerParams(vmem_limit_bytes=60 * 1024 * 1024),
        cost_estimate=pl.CostEstimate(
            flops=12 * steps * rows * width * width * chunks,
            bytes_accessed=8 << 20,
            transcendentals=steps * rows * width * chunks,
        ),
        name="sde",
    )(*operands)


def send(source, target, send_sem, recv_sem, peer):
    return pltpu.make_async_remote_copy(
        src_ref=source,
        dst_ref=target,
        send_sem=send_sem,
        recv_sem=recv_sem,
        device_id=peer,
        device_id_type=pl.DeviceIdType.MESH,
    )


def greet(peers):
    barrier = pltpu.get_barrier_semaphore()
    for peer in peers:
        pl.semaphore_signal(barrier, inc=1, device_id=peer, device_id_type=pl.DeviceIdType.MESH)
    pl.semaphore_wait(barrier, len(peers))


def mp_places():
    mine = lax.axis_index("mp")
    chip, unit = mine // 2, mine % 2
    sibling = chip * 2 + (1 - unit)
    across = (1 - chip) * 2 + unit
    diagonal = (1 - chip) * 2 + (1 - unit)
    return mine, sibling, across, diagonal


def gather_kernel(w_in_ref, w_out_ref, b_in_ref, all_in_ref, all_out_ref, all_b_ref, bias_ref, send_sem, recv_sem):
    mine, sibling, across, diagonal = mp_places()
    batch = lax.axis_index("batch")
    to_across, to_sibling = (batch, across), (batch, sibling)
    bias_ref[...] = jnp.broadcast_to(b_in_ref[...].astype(F32), bias_ref.shape)
    greet([to_across, to_sibling])
    pairs = ((w_in_ref, all_in_ref), (w_out_ref, all_out_ref), (bias_ref, all_b_ref))
    far, near, relayed = [], [], []
    for i, (own, whole) in enumerate(pairs):
        copy = send(own, whole.at[mine], send_sem.at[0, i], recv_sem.at[0, i], to_across)
        copy.start()
        far.append(copy)
    for i, (own, whole) in enumerate(pairs):
        copy = send(own, whole.at[mine], send_sem.at[1, i], recv_sem.at[1, i], to_sibling)
        copy.start()
        near.append(copy)
    for own, whole in pairs:
        whole[mine] = own[...]
    for i, (own, whole) in enumerate(pairs):
        far[i].wait_recv()
        copy = send(
            whole.at[across], whole.at[across], send_sem.at[2, i], recv_sem.at[2, i], to_sibling
        )
        copy.start()
        relayed.append(copy)
    for copy in far:
        copy.wait_send()
    for copy in near + relayed:
        copy.wait()


def gather(w_in, w_out, b_in):
    count = lax.axis_size("mp")
    vmem = pl.BlockSpec(memory_space=pltpu.VMEM)
    return pl.pallas_call(
        gather_kernel,
        out_shape=[
            jax.ShapeDtypeStruct((count,) + w_in.shape, BF16),
            jax.ShapeDtypeStruct((count,) + w_out.shape, BF16),
            jax.ShapeDtypeStruct((count, 8, b_in.shape[1]), F32),
        ],
        in_specs=[vmem] * 3,
        out_specs=[vmem] * 3,
        scratch_shapes=[
            pltpu.VMEM((8, b_in.shape[1]), F32),
            pltpu.SemaphoreType.DMA((3, 3)),
            pltpu.SemaphoreType.DMA((3, 3)),
        ],
        compiler_params=pltpu.CompilerParams(
            collective_id=0, has_side_effects=True, vmem_limit_bytes=8 * 1024 * 1024
        ),
        cost_estimate=pl.CostEstimate(flops=0, bytes_accessed=32 << 20, transcendentals=0),
        name="gather_weights",
    )(w_in, w_out, b_in)


def reduce_kernel(
    members,
    total,
    grads_ref,
    done_ref,
    decs_ref,
    near_ref,
    far_w_ref,
    far_t_ref,
    got_w_ref,
    got_t_ref,
    full_ref,
    round_ref,
    parts_ref,
    near_send,
    near_recv,
    far_send,
    far_recv,
    rs_send,
    rs_recv,
    ag_send,
    ag_recv,
    pair_send,
    pair_recv,
    dec_send,
    dec_recv,
):
    mine, sibling, across, diagonal = mp_places()
    batch = lax.axis_index("batch")
    width = grads_ref.shape[2]
    weight_rows = 2 * width
    piece = grads_ref.shape[1] // members
    others = [(lax.rem(batch + d, members), mine) for d in range(1, members)]
    group = [(batch, sibling), (batch, across), (batch, diagonal)]
    greet(group + others)
    near = []
    for i, quarter in enumerate((diagonal, sibling)):
        copy = send(
            grads_ref.at[quarter], near_ref.at[i], near_send.at[i], near_recv.at[i], group[0]
        )
        copy.start()
        near.append(copy)
    near[0].wait_recv()
    far_w_ref[...] = (
        grads_ref[across, :weight_rows, :] + near_ref[0, :weight_rows, :]
    ).astype(BF16)
    far_t_ref[...] = grads_ref[across, weight_rows:, :] + near_ref[0, weight_rows:, :]
    far = [
        send(far_w_ref, got_w_ref, far_send.at[0], far_recv.at[0], group[1]),
        send(far_t_ref, got_t_ref, far_send.at[1], far_recv.at[1], group[1]),
    ]
    for copy in far:
        copy.start()
    near[1].wait_recv()
    full_ref[...] = grads_ref[mine] + near_ref[1]
    far[0].wait_recv()
    full_ref[:weight_rows, :] += got_w_ref[...].astype(F32)
    far[1].wait_recv()
    full_ref[weight_rows:, :] += got_t_ref[...]
    for p in range(members):
        round_ref[p] = full_ref[p * piece : (p + 1) * piece, :].astype(BF16)
    scatter = []
    for d in range(1, members):
        target = lax.rem(batch + d, members)
        copy = send(
            round_ref.at[target],
            parts_ref.at[d - 1],
            rs_send.at[d - 1],
            rs_recv.at[d - 1],
            others[d - 1],
        )
        copy.start()
        scatter.append(copy)
    here = pl.ds(pl.multiple_of(batch * piece, 8), piece)
    value = full_ref[here, :]
    for d in range(1, members):
        scatter[d - 1].wait_recv()
        value = value + parts_ref[d - 1].astype(F32)
    done_ref[here, :] = value / total
    pair = batch + 1 - 2 * (batch % 2)
    partner = (pair, mine)

    def rows_of(owner):
        return done_ref.at[pl.ds(pl.multiple_of(owner * piece, 8), piece), :]

    def relay(i, owner):
        return send(rows_of(owner), rows_of(owner), pair_send.at[i], pair_recv.at[i], partner)

    hops = members // 2
    spread = []
    for d in range(1, hops):
        target = lax.rem(batch + 2 * d, members)
        copy = send(
            rows_of(batch), rows_of(batch), ag_send.at[d - 1], ag_recv.at[d - 1], (target, mine)
        )
        copy.start()
        spread.append(copy)
    passed = [relay(0, batch)]
    passed[0].start()
    for copy in near + far + scatter:
        copy.wait_send()
    for d in range(1, hops):
        origin = lax.rem(batch + members - 2 * d, members)
        send(
            rows_of(origin),
            rows_of(origin),
            ag_send.at[d - 1],
            ag_recv.at[d - 1],
            (origin, mine),
        ).wait_recv()
        copy = relay(d, origin)
        copy.start()
        passed.append(copy)
    for d in range(hops):
        relay(d, lax.rem(pair + members - 2 * d, members)).wait_recv()
    spread += passed
    dec_rows = decs_ref.shape[1]
    exchange = []
    for i in range(3):
        copy = send(
            done_ref.at[pl.ds(weight_rows, dec_rows), :],
            decs_ref.at[mine],
            dec_send.at[i],
            dec_recv.at[i],
            group[i],
        )
        copy.start()
        exchange.append(copy)
    decs_ref[mine] = done_ref[weight_rows : weight_rows + dec_rows, :]
    for copy in spread:
        copy.wait_send()
    for i, origin in enumerate((sibling, across, diagonal)):
        exchange[i].wait_send()
        send(
            decs_ref.at[origin], decs_ref.at[origin], dec_send.at[i], dec_recv.at[i], group[i]
        ).wait_recv()


def finish_kernel(
    half, done_ref, decs_ref, w_in_ref, w_out_ref, b_in_ref, b_out_ref, dec_ref, scores_ref
):
    width = done_ref.shape[1]
    weight_rows = 2 * width
    dec_rows = decs_ref.shape[1]
    line = weight_rows + dec_rows
    w_in_ref[...] = done_ref[:width, :]
    w_out_ref[...] = done_ref[width:weight_rows, :]
    b_in_ref[...] = done_ref[line : line + 1, :]
    b_out_ref[...] = done_ref[line + 1 : line + 2, :]
    scores_ref[:, 0:1] = jnp.sum(done_ref[line + 2 : line + 3, :half], axis=1, keepdims=True)
    scores_ref[:, 1:2] = jnp.sum(
        done_ref[line + 2 : line + 3, half : 2 * half], axis=1, keepdims=True
    )
    seen_width = dec_ref.shape[1]
    for n in range(decs_ref.shape[0]):
        for m in range(width // seen_width):
            start = (n * (width // seen_width) + m) * dec_rows
            dec_ref[start : start + dec_rows, :] = decs_ref[
                n, :, m * seen_width : (m + 1) * seen_width
            ]


def reduce_all(grads, rows, seen_width):
    quarters, grad_rows, width = grads.shape
    members = lax.axis_size("batch")
    total = rows * members * lax.axis_size("mp")
    dec_rows = width // quarters // (width // seen_width)
    tail_rows = grad_rows - 2 * width
    piece = grad_rows // members
    vmem = pl.BlockSpec(memory_space=pltpu.VMEM)
    sems = []
    for count in (2, 2, members - 1, members // 2, members // 2, 3):
        sems += [pltpu.SemaphoreType.DMA((count,))] * 2

    def body(*refs):
        reduce_kernel(members, total, *refs)

    done, decs = pl.pallas_call(
        body,
        out_shape=[
            jax.ShapeDtypeStruct((grad_rows, width), F32),
            jax.ShapeDtypeStruct((quarters, dec_rows, width), F32),
        ],
        in_specs=[vmem],
        out_specs=[vmem] * 2,
        scratch_shapes=[
            pltpu.VMEM((2, grad_rows, width), F32),
            pltpu.VMEM((2 * width, width), BF16),
            pltpu.VMEM((tail_rows, width), F32),
            pltpu.VMEM((2 * width, width), BF16),
            pltpu.VMEM((tail_rows, width), F32),
            pltpu.VMEM((grad_rows, width), F32),
            pltpu.VMEM((members, piece, width), BF16),
            pltpu.VMEM((members - 1, piece, width), BF16),
        ]
        + sems,
        compiler_params=pltpu.CompilerParams(
            collective_id=1, has_side_effects=True, vmem_limit_bytes=16 * 1024 * 1024
        ),
        name="reduce_grads",
    )(grads)

    def finish(*refs):
        finish_kernel(rows, *refs)

    return pl.pallas_call(
        finish,
        out_shape=[
            jax.ShapeDtypeStruct((width, width), F32),
            jax.ShapeDtypeStruct((width, width), F32),
            jax.ShapeDtypeStruct((1, width), F32),
            jax.ShapeDtypeStruct((1, width), F32),
            jax.ShapeDtypeStruct((width, seen_width), F32),
            jax.ShapeDtypeStruct((1, 2), F32),
        ],
        in_specs=[vmem] * 2,
        out_specs=[vmem] * 6,
        compiler_params=pltpu.CompilerParams(vmem_limit_bytes=8 * 1024 * 1024),
        name="finish",
    )(done, decs)


def on_device(
    init_state,
    brownian,
    step_size,
    lengths,
    obs_steps,
    observed,
    w_in,
    b_in,
    w_out,
    b_out,
    decoder,
    prior_rate,
    diffusion,
):
    rows, width = init_state.shape
    seen_width = decoder.shape[1]
    w_in_all, w_out_all, b_in_all = gather(w_in, w_out, b_in[None, :])
    unit = 8 * lax.axis_size("batch")
    need = 2 * width + width // lax.axis_size("mp") * seen_width // width + 3
    elbo, grads, cot = core(
        -(-need // unit) * unit,
        init_state,
        brownian,
        step_size[None, :],
        lengths[None, :],
        obs_steps.T,
        observed,
        w_in_all,
        b_in_all,
        w_out_all,
        b_out[None, :],
        decoder,
        prior_rate[None, :],
        diffusion[None, :],
    )
    own_w_in, own_w_out, own_b_in, b_out_grad, dec_grad, scores = reduce_all(
        grads, rows, seen_width
    )
    return (
        elbo[0],
        scores[0],
        own_w_in,
        own_b_in[0],
        own_w_out,
        b_out_grad[0],
        dec_grad,
        cot,
    )


def solution(mesh):
    both = ("batch", "mp")
    placed = (
        P(both, None),
        P(None, both, None),
        P(both),
        P(both),
        P(both, None),
        P(both, None, None),
        P(None, "mp"),
        P("mp"),
        P("mp", None),
        P(),
        P(),
        P(),
        P(),
    )
    return jax.shard_map(
        on_device,
        mesh=mesh,
        in_specs=placed,
        out_specs=(
            P(both),
            P(),
            P(None, "mp"),
            P("mp"),
            P("mp", None),
            P(),
            P(),
            P(both, None),
        ),
        check_vma=False,
    )
```

profile of v0, /device:TPU:1, one launch (start us, length us, event | category | flops | bytes accessed | tf_op | source)
XLA Modules:
  0.0 155.9 jit_solution(18292576018094384472)
XLA Ops:
  0.6 0.7 broadcast_in_dim.20.b_in_ref
  1.3 0.0 copy-start.1
  1.3 0.9 copy-done.1
  2.2 0.0 copy-start.2
  2.2 0.9 copy-done.2
  3.1 21.5 %gather_weights.1 = (bf16[4,256,256]{2,1,0:T(8,128)(2,1)S(1)}, bf16[4,256,256]{2,1,0:T(8,128)(2,1)S(1)}, f32[4,8,256]{2,1,0:T(8,128)S(1)}) custom-call(bf16[256,256]{1,0:T(8,128)(2,1)S(1)} %copy-done.1, bf16[256,256]{1,0:T(8,128)(2,1)S(1)} %copy-done.2, bf16[1,256]{1,0:T(2,128)(2,1)S(1)} %broadcast_in_dim.20.b_in_ref), custom_call_target="tpu_custom_call" | custom-call | bytes 33554432 | tf_op jit(solution)/shard_map/gather_weights/pallas_call | solution.py:326
  24.6 0.0 copy-start.3
  24.6 0.8 copy-done.3
  25.4 0.0 copy-start.4
  25.4 0.8 copy-done.4
  26.2 0.0 copy-start.5
  26.2 0.6 copy-done.5
  26.8 49.9 %sde.1 = (f32[1,128]{1,0:T(1,128)}, f32[4,768,256]{2,1,0:T(8,128)}, f32[128,256]{1,0:T(8,128)}) custom-call(f32[128,256]{1,0:T(8,128)} %refs_0_.1, bf16[32,128,256]{2,1,0:T(8,128)(2,1)} %refs_1_.1, f32[1,128]{1,0:T(1,128)} %bitcast.16, s32[1,128]{1,0:T(1,128)} %bitcast.17, s32[8,128]{1,0:T(8,128)} %bitcast.10, bf16[128,8,128]{2,1,0:T(8,128)(2,1)} %refs_5_.1, ...), custom_call_target="tpu_custom_call" | custom-call | flops 12884901888 | bytes 8388608 | tf_op jit(solution)/shard_map/sde/pallas_call | solution.py:249
  76.8 0.0 copy-start
  76.8 1.9 %copy-done = f32[4,768,256]{2,1,0:T(8,128)S(1)} copy-done((f32[4,768,256]{2,1,0:T(8,128)S(1)}, f32[4,768,256]{2,1,0:T(8,128)}, u32[]{:S(2)}) %copy-start) | copy-done | bytes 3145752
  78.7 76.4 %reduce_grads.1 = (f32[768,256]{1,0:T(8,128)S(1)}, f32[4,32,256]{2,1,0:T(8,128)S(1)}) custom-call(f32[4,768,256]{2,1,0:T(8,128)S(1)} %copy-done), custom_call_target="tpu_custom_call" | custom-call | tf_op jit(solution)/shard_map/reduce_grads/pallas_call | solution.py:525
  155.0 0.9 finish.1
Async XLA Ops:
  1.3 0.9 copy-start.1
  2.2 0.9 copy-start.2
  24.6 0.8 copy-start.3
  25.4 0.8 copy-start.4
  26.2 0.6 copy-start.5
  76.8 1.9 %copy-start = (f32[4,768,256]{2,1,0:T(8,128)S(1)}, f32[4,768,256]{2,1,0:T(8,128)}, u32[]{:S(2)}) copy-start(f32[4,768,256]{2,1,0:T(8,128)} %get-tuple-element.26.refs_0_) | copy-start | bytes 9437188
where the time goes:
time: 156 us
  Pallas kernels  149 us (96%)
  local copies, waits for them, and re-layouts  6.54 us (4%)
    pallas_call x1, Pallas kernels, reduce_all(): pl.pallas_call(body, out_shape=[jax.ShapeDtypeStruct((grad_rows, width),...  76.4 us
    pallas_call x1, Pallas kernels, core(): pl.pallas_call(body, out_shape=out, in_specs=specs, out_specs=[vmem] * 3,...  49.9 us
    pallas_call x1, Pallas kernels, gather(): pl.pallas_call(gather_kernel, out_shape=[jax.ShapeDtypeStruct((count,) +...  21.5 us
    unnamed x12, local copies, waits for them, and re-layouts  5.88 us

commit v1 on v0

v1 whole, which is shorter than its diff:
```python
import types

import jax
import jax.numpy as jnp
from jax import lax
from jax.experimental import pallas as pl
from jax.experimental.pallas import tpu as pltpu
from jax.sharding import PartitionSpec as P

F32 = jnp.float32
BF16 = jnp.bfloat16


def dot(a, b):
    return jnp.dot(a, b, preferred_element_type=F32)


def fold(value):
    return value.reshape(-1, 8, value.shape[1]).sum(axis=0)


def send(source, target, sems, at, peer):
    return pltpu.make_async_remote_copy(
        src_ref=source,
        dst_ref=target,
        send_sem=sems[0].at[at],
        recv_sem=sems[1].at[at],
        device_id=peer,
        device_id_type=pl.DeviceIdType.MESH,
    )


OPERANDS = (
    "init",
    "noise",
    "step",
    "length",
    "obs",
    "seen",
    "w_in",
    "b_in",
    "w_out",
    "b_out",
    "dec",
    "rate",
    "diff",
)
EXCHANGES = ("w_far", "w_near", "b_far")


def fused_kernel(sizes, r):
    rows, width, steps = sizes.rows, sizes.width, sizes.steps
    seen_count, seen_width = sizes.seen_count, sizes.seen_width
    quarters, planes, total = sizes.quarters, sizes.planes, sizes.total
    mine = lax.axis_index("mp")
    batch = lax.axis_index("batch")
    core = lax.rem(batch, 2)
    other = 1 - core
    place = lax.div(batch, 2)
    sibling = (batch + 1 - 2 * core, mine)

    def quarter_at(d):
        return lax.rem(mine + d, quarters)

    def line_peer(d):
        return (batch, quarter_at(d))

    def place_at(d):
        return lax.rem(place + d, planes)

    def plane_peer(d):
        return (2 * place_at(d) + core, mine)

    far = [2, 1, 3] if quarters == 4 else list(range(1, quarters))

    weights = [
        pltpu.make_async_copy(r.w_in_hbm, r.all_w.at[0, mine], r.load_sem.at[0]),
        pltpu.make_async_copy(r.w_out_hbm, r.all_w.at[1, mine], r.load_sem.at[1]),
        pltpu.make_async_copy(r.b_in_hbm, r.b_own, r.load_sem.at[2]),
    ]
    for copy in weights:
        copy.start()
    loads = []
    for name in OPERANDS:
        if name in ("w_in", "w_out", "b_in"):
            continue
        copy = pltpu.make_async_copy(
            getattr(r, name + "_hbm"), getattr(r, name), r.load_sem.at[3 + len(loads)]
        )
        copy.start()
        loads.append(copy)

    barrier = pltpu.get_barrier_semaphore()
    peers = [sibling] + [line_peer(d) for d in range(1, quarters)]
    peers += [plane_peer(d) for d in range(1, planes)]
    for peer in peers:
        pl.semaphore_signal(barrier, inc=1, device_id=peer, device_id_type=pl.DeviceIdType.MESH)
    for copy in weights:
        copy.wait()
    r.all_b[mine] = jnp.broadcast_to(r.b_own[...].astype(F32), (8, width))
    pl.semaphore_wait(barrier, len(peers))

    sent = []
    for d in far:
        own = r.all_w.at[core, mine]
        copy = send(own, own, r.w_far, d - 1, line_peer(d))
        copy.start()
        sent.append(copy)
    for d in far:
        own = r.all_b.at[mine]
        copy = send(own, own, r.b_far, d - 1, line_peer(d))
        copy.start()
        sent.append(copy)

    def column(row):
        return jnp.broadcast_to(row, (rows, rows)).T

    for copy in loads:
        copy.wait()
    r.dt[...] = column(r.step[...])
    r.root[...] = jnp.sqrt(r.dt[...])
    r.len[...] = column(r.length[...])
    for j in range(seen_count):
        r.obs_wide[j] = column(r.obs[j : j + 1, :])
    r.target[...] = r.seen[...].astype(F32).reshape(r.target.shape)
    r.pick[...] = jnp.zeros_like(r.pick)
    r.kl[...] = jnp.zeros_like(r.kl)
    r.sum_b_in[...] = jnp.zeros_like(r.sum_b_in)
    r.sum_b_out[...] = jnp.zeros_like(r.sum_b_out)
    r.state[...] = r.init[...]
    r.x[0] = r.init[...].astype(BF16)
    dec_t = r.dec[...].T
    r.dec_t[:seen_width, :] = dec_t
    r.dec_t[seen_width:, :] = dec_t

    order = [1, 3, 2] if quarters == 4 else list(range(1, quarters))
    for d in order:
        origin = quarter_at(quarters - d)
        got = r.all_w.at[core, origin]
        send(got, got, r.w_far, d - 1, line_peer(d)).wait_recv()
        copy = send(got, got, r.w_near, d - 1, sibling)
        copy.start()
        sent.append(copy)
    for d in order:
        origin = quarter_at(quarters - d)
        got = r.all_b.at[origin]
        send(got, got, r.b_far, d - 1, line_peer(d)).wait_recv()
        got = r.all_w.at[other, origin]
        send(got, got, r.w_near, d - 1, sibling).wait_recv()
    for copy in sent:
        copy.wait_send()

    def both(value):
        return jnp.concatenate([value] * (width // rows), axis=1)

    def look(k, x):
        seen = dot(x, r.dec[...])
        for j in range(seen_count):
            r.pick[j] = jnp.where(r.obs_wide[j] == k, seen, r.pick[j])

    def turn(k, x):
        r.xt[:, pl.ds(pl.multiple_of(k * rows, rows), rows)] = x.T

    def forward(k, carry):
        x = r.x[k]
        drift = jnp.broadcast_to(r.b_out[...], (rows, width))
        for n in range(quarters):
            act = jnp.tanh(dot(x, r.all_w[0, n]) + r.all_b[n, :1, :]).astype(BF16)
            r.act[n, pl.ds(k * rows, rows), :] = act
            drift = drift + dot(act, r.all_w[1, n])
        state = r.state[...]
        inv = 1.0 / r.diff[...]
        live = k < r.len[...]
        factor = both(jnp.where(live, r.dt[...], 0.0))
        root = both(jnp.where(live, r.root[...], 0.0))
        following = state + (
            factor * drift + r.diff[...] * root * r.noise[k].astype(F32)
        )
        r.state[...] = following
        r.x[k + 1] = following.astype(BF16)
        residual = (drift + r.rate[...] * state) * inv
        r.kl[...] += factor * residual * residual
        r.scaled[k] = residual * inv
        turn(k, x)
        look(k, x)
        which = lax.rem(k, 2 * quarters)
        tensor, n = lax.div(which, quarters), lax.rem(which, quarters)
        r.all_t[tensor, n] = r.all_w[tensor, n].T
        return carry

    lax.fori_loop(0, steps, forward, 0)
    look(steps, r.x[steps])
    turn(steps, r.x[steps])

    square = jnp.zeros((rows, seen_width), F32)
    for j in range(seen_count):
        misfit = r.pick[j] - r.target[pl.ds(j, rows, stride=seen_count), :]
        square = square + misfit * misfit
        r.pick[j] = misfit.astype(BF16).astype(F32)
    loglik = -0.5 * jnp.sum(square.T, axis=0, keepdims=True)
    kl_half = r.kl[:, :rows]
    for part in range(1, width // rows):
        kl_half = kl_half + r.kl[:, part * rows : (part + 1) * rows]
    kl_row = 0.5 * jnp.sum(kl_half.T, axis=0, keepdims=True)
    divisor = (width * r.length[...] + seen_width * seen_count).astype(F32)
    r.elbo_out[...] = (loglik - kl_row) / divisor

    def observe(t):
        spread = jnp.zeros((rows, seen_width), F32)
        for j in range(seen_count):
            spread = spread + jnp.where(r.obs_wide[j] == t, r.pick[j], 0.0)
        high = spread.astype(BF16)
        low = (spread - high.astype(F32)).astype(BF16)
        pair = jnp.concatenate([high, low], axis=1)
        r.miss[pl.ds(t * rows, rows), :] = pair
        r.obs_back[...] = dot(pair, r.dec_t[...])

    observe(steps)
    r.cot[...] = jnp.zeros_like(r.cot)

    def backward(index, carry):
        k = steps - 1 - index
        cot = r.cot[...] + r.obs_back[...]
        scaled = r.scaled[k]
        factor = both(jnp.where(k < r.len[...], r.dt[...], 0.0))
        update = factor * (cot + scaled)
        rounded = update.astype(BF16)
        cot = cot + factor * r.rate[...] * scaled
        for n in range(quarters):
            act = r.act[n, pl.ds(k * rows, rows), :].astype(F32)
            pre = dot(rounded, r.all_t[1, n]) * (1.0 - act * act)
            pre_round = pre.astype(BF16)
            cot = cot + dot(pre_round, r.all_t[0, n])
            r.pre[n, pl.ds(k * rows, rows), :] = pre_round
            r.sum_b_in[n] += fold(pre)
        r.cot[...] = cot
        r.ut[:, pl.ds(pl.multiple_of(k * rows, rows), rows)] = rounded.T
        r.sum_b_out[...] += fold(update)
        observe(k)
        return carry

    lax.fori_loop(0, steps, backward, 0)
    r.cot_out[...] = r.cot[...]

    for n in range(quarters):
        r.tail[n : n + 1, :] = jnp.sum(r.sum_b_in[n], axis=0, keepdims=True)
    r.tail[quarters : quarters + 1, :] = jnp.sum(r.sum_b_out[...], axis=0, keepdims=True)
    r.tail[quarters + 1 : quarters + 2, :rows] = loglik
    r.tail[quarters + 1 : quarters + 2, rows : 2 * rows] = kl_row
    r.tail[quarters + 2 :, :] = jnp.zeros((r.tail.shape[0] - quarters - 2, width), F32)
    tail_near = send(r.tail, r.tail_sib, r.near, 0, sibling)
    tail_near.start()
    waits = [tail_near]
    dec_grad = dot(r.xt[:, rows:], r.miss[rows:, :])
    dec_grad = dec_grad[:, :seen_width] + dec_grad[:, seen_width:]
    r.dec_part[...] = dec_grad.reshape(r.dec_part.shape)
    dec_near = send(r.dec_part.at[other], r.dec_sib, r.near, 1, sibling)
    dec_near.start()
    waits.append(dec_near)
    dec_rows = r.dec_sum.shape[1]

    def chunk(i, d):
        n = quarter_at(d)
        r.grad[i, 0] = dot(r.xt[:, : steps * rows], r.pre[n])
        r.grad[i, 1] = dot(r.ut[...], r.act[n]).T
        copy = send(r.grad.at[i, other], r.grad_sib.at[i], r.near, 3 + i, sibling)
        copy.start()
        waits.append(copy)
        return copy

    def joined(i, copy):
        copy.wait_recv()
        return r.grad[i, core] + r.grad_sib[i]

    def pass_on(i, d, copy):
        r.line_out[i] = joined(i, copy).astype(BF16)
        moved = send(r.line_out.at[i], r.line_in.at[i], r.line, i, line_peer(d))
        moved.start()
        waits.append(moved)
        return moved

    passed = []
    for i, d in enumerate(far):
        near = chunk(i, d)
        if i == 0:
            tail_near.wait_recv()
            r.tail_sum[...] = r.tail[...] + r.tail_sib[...]
            dec_near.wait_recv()
            r.dec_sum[...] = (r.dec_part[core] + r.dec_sib[...]).reshape(r.dec_sum.shape)
            tail_plane, dec_plane = [], []
            for e in range(1, planes):
                copy = send(r.tail_sum, r.tail_in.at[e - 1], r.tail_plane, e - 1, plane_peer(e))
                copy.start()
                tail_plane.append(copy)
                copy = send(
                    r.dec_sum.at[place_at(e)],
                    r.dec_in.at[e - 1],
                    r.dec_plane,
                    e - 1,
                    plane_peer(e),
                )
                copy.start()
                dec_plane.append(copy)
            waits += tail_plane + dec_plane
        if i == 1:
            value = r.tail_sum[...]
            for e in range(1, planes):
                tail_plane[e - 1].wait_recv()
                value = value + r.tail_in[e - 1]
            r.tail_line[...] = value
            value = r.dec_sum[place]
            for e in range(1, planes):
                dec_plane[e - 1].wait_recv()
                value = value + r.dec_in[e - 1]
            r.dec_line[...] = value
            tail_far, dec_far = [], []
            for e in range(1, quarters):
                copy = send(
                    r.tail_line, r.tail_line_in.at[e - 1], r.tail_far, e - 1, line_peer(e)
                )
                copy.start()
                tail_far.append(copy)
                copy = send(r.dec_line, r.dec_line_in.at[e - 1], r.dec_far, e - 1, line_peer(e))
                copy.start()
                dec_far.append(copy)
            waits += tail_far + dec_far
        if i == 2:
            value = r.tail_line[...]
            for e in range(1, quarters):
                tail_far[e - 1].wait_recv()
                value = value + r.tail_line_in[e - 1]
            r.tail_total[...] = value
            value = r.dec_line[...]
            for e in range(1, quarters):
                dec_far[e - 1].wait_recv()
                value = value + r.dec_line_in[e - 1]
            r.dec_all[core, place] = value / total
            own = r.dec_all.at[core, place]
            for e in range(1, planes):
                copy = send(own, own, r.dec_spread, e - 1, plane_peer(e))
                copy.start()
                waits.append(copy)
        passed.append(pass_on(i, d, near))

    last = len(far)
    near = chunk(last, 0)
    for e in range(1, planes):
        got = r.dec_all.at[core, place_at(planes - e)]
        send(got, got, r.dec_spread, e - 1, plane_peer(e)).wait_recv()
    dec_hand = send(r.dec_all.at[core], r.dec_all.at[core], r.near, 2, sibling)
    dec_hand.start()
    value = joined(last, near)
    for i in range(last):
        passed[i].wait_recv()
        value = value + r.line_in[i].astype(F32)
    r.full[...] = value
    r.plane_out[...] = value.astype(BF16).reshape(r.plane_out.shape)
    plane = []
    for e in range(1, planes):
        copy = send(
            r.plane_out.at[place_at(e)], r.plane_in.at[e - 1], r.plane, e - 1, plane_peer(e)
        )
        copy.start()
        plane.append(copy)
    waits += plane
    piece = width // planes

    def rows_of(tensor, owner):
        return r.res_out.at[tensor, pl.ds(pl.multiple_of(owner * piece, piece), piece), :]

    value = r.full[pl.ds(pl.multiple_of(place * piece, piece), piece), :]
    for e in range(1, planes):
        plane[e - 1].wait_recv()
        value = value + r.plane_in[e - 1].astype(F32)
    r.res_out[core, pl.ds(pl.multiple_of(place * piece, piece), piece), :] = value / total
    own = rows_of(core, place)
    for e in range(1, planes):
        copy = send(own, own, r.spread, e - 1, plane_peer(e))
        copy.start()
        waits.append(copy)
    copy = send(own, own, r.hand, 0, sibling)
    copy.start()
    waits.append(copy)
    for e in range(1, planes):
        got = rows_of(core, place_at(planes - e))
        send(got, got, r.spread, e - 1, plane_peer(e)).wait_recv()
        copy = send(got, got, r.hand, e, sibling)
        copy.start()
        waits.append(copy)
    got = r.dec_all.at[other]
    send(got, got, r.near, 2, sibling).wait_recv()
    r.dec_out[...] = r.dec_all[...].reshape(r.dec_out.shape)
    scale = 1.0 / total
    r.tail_out[0:1, :] = r.tail_total[pl.ds(mine, 1), :] * scale
    r.tail_out[1:3, :] = r.tail_total[quarters : quarters + 2, :] * scale
    r.tail_out[3:, :] = jnp.zeros((r.tail_out.shape[0] - 3, width), F32)
    for copy in waits:
        copy.wait_send()
    dec_hand.wait_send()
    for e in range(planes):
        got = rows_of(other, place_at(planes - e) if e else place)
        send(got, got, r.hand, e, sibling).wait_recv()


def fused(sizes, operands):
    rows, width, steps = sizes.rows, sizes.width, sizes.steps
    count, seen_width = sizes.seen_count, sizes.seen_width
    quarters, planes = sizes.quarters, sizes.planes
    piece = width // planes
    dec_rows = width // 2 // planes
    outs = {
        "elbo_out": ((1, rows), F32),
        "res_out": ((2, width, width), F32),
        "tail_out": ((8, width), F32),
        "dec_out": ((width, seen_width), F32),
        "cot_out": ((rows, width), F32),
    }
    arrays = {
        "x": ((steps + 1, rows, width), BF16),
        "xt": ((width, (steps + 1) * rows), BF16),
        "ut": ((width, steps * rows), BF16),
        "act": ((quarters, steps * rows, width), BF16),
        "pre": ((quarters, steps * rows, width), BF16),
        "scaled": ((steps, rows, width), F32),
        "pick": ((count, rows, seen_width), F32),
        "obs_wide": ((count, rows, rows), jnp.int32),
        "dt": ((rows, rows), F32),
        "root": ((rows, rows), F32),
        "len": ((rows, rows), jnp.int32),
        "state": ((rows, width), F32),
        "kl": ((rows, width), F32),
        "cot": ((rows, width), F32),
        "obs_back": ((rows, width), F32),
        "sum_b_in": ((quarters, 8, width), F32),
        "sum_b_out": ((8, width), F32),
        "miss": (((steps + 1) * rows, 2 * seen_width), BF16),
        "target": ((rows * count, seen_width), F32),
        "all_w": ((2, quarters, width, width), BF16),
        "all_t": ((2, quarters, width, width), BF16),
        "all_b": ((quarters, 8, width), F32),
        "b_own": (sizes.b_shape, BF16),
        "dec_t": ((2 * seen_width, width), BF16),
        "tail": ((8, width), F32),
        "tail_sib": ((8, width), F32),
        "tail_sum": ((8, width), F32),
        "tail_in": ((planes - 1, 8, width), F32),
        "tail_line": ((8, width), F32),
        "tail_total": ((8, width), F32),
        "tail_line_in": ((quarters - 1, 8, width), F32),
        "dec_part": ((2, width // 2, seen_width), F32),
        "dec_sib": ((width // 2, seen_width), F32),
        "dec_sum": ((planes, dec_rows, seen_width), F32),
        "dec_in": ((planes - 1, dec_rows, seen_width), F32),
        "dec_line": ((dec_rows, seen_width), F32),
        "dec_line_in": ((quarters - 1, dec_rows, seen_width), F32),
        "dec_all": ((2, planes, dec_rows, seen_width), F32),
        "grad": ((quarters, 2, width, width), F32),
        "grad_sib": ((quarters, width, width), F32),
        "line_out": ((quarters - 1, width, width), BF16),
        "line_in": ((quarters - 1, width, width), BF16),
        "full": ((width, width), F32),
        "plane_out": ((planes, piece, width), BF16),
        "plane_in": ((planes - 1, piece, width), BF16),
    }
    for name, value in zip(OPERANDS, operands):
        if name not in ("w_in", "w_out", "b_in"):
            arrays[name] = (value.shape, value.dtype)
    links = {
        "w_far": quarters - 1,
        "w_near": quarters - 1,
        "b_far": quarters - 1,
        "near": 3 + quarters,
        "line": quarters - 1,
        "tail_plane": planes - 1,
        "dec_plane": planes - 1,
        "tail_far": quarters - 1,
        "dec_far": quarters - 1,
        "dec_spread": planes - 1,
        "plane": planes - 1,
        "spread": planes - 1,
        "hand": planes,
    }
    scratch = [pltpu.VMEM(shape, dtype) for shape, dtype in arrays.values()]
    for number in links.values():
        scratch += [pltpu.SemaphoreType.DMA((number,))] * 2
    scratch.append(pltpu.SemaphoreType.DMA((len(OPERANDS),)))

    def body(*refs):
        refs = list(refs)
        r = types.SimpleNamespace()
        for name in OPERANDS:
            setattr(r, name + "_hbm", refs.pop(0))
        for name in list(outs) + list(arrays):
            setattr(r, name, refs.pop(0))
        for name in links:
            setattr(r, name, (refs.pop(0), refs.pop(0)))
        r.load_sem = refs.pop(0)
        fused_kernel(sizes, r)

    return pl.pallas_call(
        body,
        out_shape=[jax.ShapeDtypeStruct(shape, dtype) for shape, dtype in outs.values()],
        in_specs=[pl.BlockSpec(memory_space=pltpu.HBM)] * len(OPERANDS),
        out_specs=[pl.BlockSpec(memory_space=pltpu.VMEM)] * len(outs),
        scratch_shapes=scratch,
        compiler_params=pltpu.CompilerParams(
            collective_id=0, has_side_effects=True, vmem_limit_bytes=60 * 1024 * 1024
        ),
        name="fused",
    )(*operands)


def finish_kernel(half, res_ref, tail_ref, dec_in, cot_in, elbo_in, w_in, w_out, b_in, b_out, dec, scores, cot, elbo):
    w_in[...] = res_ref[0]
    w_out[...] = res_ref[1]
    b_in[...] = tail_ref[0:1, :]
    b_out[...] = tail_ref[1:2, :]
    scores[:, 0:1] = jnp.sum(tail_ref[2:3, :half], axis=1, keepdims=True)
    scores[:, 1:2] = jnp.sum(tail_ref[2:3, half : 2 * half], axis=1, keepdims=True)
    dec[...] = dec_in[...]
    cot[...] = cot_in[...]
    elbo[...] = elbo_in[...]


def finish(rows, res, tail, dec, cot, elbo):
    width, seen_width = dec.shape
    shapes = [
        (width, width),
        (width, width),
        (1, width),
        (1, width),
        dec.shape,
        (1, 2),
        cot.shape,
        elbo.shape,
    ]

    def body(*refs):
        finish_kernel(rows, *refs)

    vmem = pl.BlockSpec(memory_space=pltpu.VMEM)
    return pl.pallas_call(
        body,
        out_shape=[jax.ShapeDtypeStruct(shape, F32) for shape in shapes],
        in_specs=[vmem] * 5,
        out_specs=[vmem] * len(shapes),
        compiler_params=pltpu.CompilerParams(vmem_limit_bytes=8 * 1024 * 1024),
        name="finish",
    )(res, tail, dec, cot, elbo)


def on_device(
    init_state,
    brownian,
    step_size,
    lengths,
    obs_steps,
    observed,
    w_in,
    b_in,
    w_out,
    b_out,
    decoder,
    prior_rate,
    diffusion,
):
    rows, width = init_state.shape
    quarters = lax.axis_size("mp")
    members = lax.axis_size("batch")
    sizes = types.SimpleNamespace(
        rows=rows,
        width=width,
        steps=brownian.shape[0],
        seen_count=observed.shape[1],
        seen_width=observed.shape[2],
        quarters=quarters,
        planes=members // 2,
        total=rows * members * quarters,
        b_shape=(1, b_in.shape[0]),
    )
    elbo, res, tail, dec, cot = fused(
        sizes,
        (
            init_state,
            brownian,
            step_size[None, :],
            lengths[None, :],
            obs_steps.T,
            observed,
            w_in,
            b_in[None, :],
            w_out,
            b_out[None, :],
            decoder,
            prior_rate[None, :],
            diffusion[None, :],
        ),
    )
    own_w_in, own_w_out, own_b_in, b_out_grad, dec_grad, scores, cot, elbo = finish(
        rows, res, tail, dec, cot, elbo
    )
    return (
        elbo[0],
        scores[0],
        own_w_in,
        own_b_in[0],
        own_w_out,
        b_out_grad[0],
        dec_grad,
        cot,
    )


def solution(mesh):
    both = ("batch", "mp")
    placed = (
        P(both, None),
        P(None, both, None),
        P(both),
        P(both),
        P(both, None),
        P(both, None, None),
        P(None, "mp"),
        P("mp"),
        P("mp", None),
        P(),
        P(),
        P(),
        P(),
    )
    return jax.shard_map(
        on_device,
        mesh=mesh,
        in_specs=placed,
        out_specs=(
            P(both),
            P(),
            P(None, "mp"),
            P("mp"),
            P("mp", None),
            P(),
            P(),
            P(both, None),
        ),
        check_vma=False,
    )
```

time: 156 us -> 87.2 us (0.56)
  Pallas kernels: 149 us -> 80.9 us
    pallas_call x4 -> x2, Pallas kernels: 149 us -> 80.9 us  [the longest x1 80 us: fused(): pl.pallas_call(body, out_shape=[jax.ShapeDtypeStruct(shape, dtype) for sh...]
    unnamed x12 -> x10, local copies, waits for them, and re-layouts: 5.88 us -> 4.17 us
where the time goes in v1:
time: 87.2 us; the launch traced here: 86.9 us
  Pallas kernels  80.9 us (93%)
  local copies, waits for them, and re-layouts  5.39 us (6%)
    pallas_call x1, Pallas kernels, fused(): pl.pallas_call(body, out_shape=[jax.ShapeDtypeStruct(shape, dtype) for sh...  80 us
    unnamed x10, local copies, waits for them, and re-layouts  4.17 us

profile of v1, /device:TPU:1, one launch (start us, length us, event | category | flops | bytes accessed | tf_op | source)
XLA Modules:
  0.0 86.9 jit_solution(13310352635980754846)
XLA Ops:
  0.6 1.2 %broadcast_in_dim.20.refs_7_ = bf16[1,256]{1,0:T(2,128)(2,1)} reshape(bf16[256]{0:T(256)(128)(2,1)} %param.20) | data formatting | bytes 1024 | tf_op jit(solution)/shard_map/broadcast_in_dim | solution.py:591
  1.9 80.0 %fused.1 = (f32[1,128]{1,0:T(1,128)}, f32[2,256,256]{2,1,0:T(8,128)}, f32[8,256]{1,0:T(8,128)}, f32[256,128]{1,0:T(8,128)}, f32[128,256]{1,0:T(8,128)}) custom-call(f32[128,256]{1,0:T(8,128)} %refs_0_.1, bf16[32,128,256]{2,1,0:T(8,128)(2,1)} %refs_1_.1, f32[1,128]{1,0:T(1,128)} %bitcast.14, s32[1,128]{1,0:T(1,128)} %bitcast.15, s32[8,128]{1,0:T(8,128)} %bitcast.10, ...), custom_call_target="tpu_custom_call" | custom-call | tf_op jit(solution)/shard_map/fused/pallas_call | solution.py:500
  81.9 0.0 copy-start
  81.9 1.0 %copy-done = f32[2,256,256]{2,1,0:T(8,128)S(1)} copy-done((f32[2,256,256]{2,1,0:T(8,128)S(1)}, f32[2,256,256]{2,1,0:T(8,128)}, u32[]{:S(2)}) %copy-start) | copy-done | bytes 524312
  82.9 0.0 copy-start.1
  82.9 0.9 %copy-done.1 = f32[256,128]{1,0:T(8,128)S(1)} copy-done((f32[256,128]{1,0:T(8,128)S(1)}, f32[256,128]{1,0:T(8,128)}, u32[]{:S(2)}) %copy-start.1) | copy-done | bytes 131096
  83.8 0.0 copy-start.2
  83.8 0.9 %copy-done.2 = f32[128,256]{1,0:T(8,128)S(1)} copy-done((f32[128,256]{1,0:T(8,128)S(1)}, f32[128,256]{1,0:T(8,128)}, u32[]{:S(2)}) %copy-start.2) | copy-done | bytes 131096
  84.7 0.0 copy-start.3
  84.7 0.7 copy-done.3
  85.4 0.0 copy-start.4
  85.4 0.6 copy-done.4
  86.0 0.9 %finish.1 = (f32[256,256]{1,0:T(8,128)}, f32[256,256]{1,0:T(8,128)}, f32[1,256]{1,0:T(1,128)}, f32[1,256]{1,0:T(1,128)}, f32[256,128]{1,0:T(8,128)}, /*index=5*/...) custom-call(f32[2,256,256]{2,1,0:T(8,128)S(1)} %copy-done, f32[8,256]{1,0:T(8,128)S(1)} %copy-done.3, ...), custom_call_target="tpu_custom_call" | custom-call | tf_op jit(solution)/shard_map/finish/pallas_call | solution.py:542
Async XLA Ops:
  81.9 1.0 %copy-start = (f32[2,256,256]{2,1,0:T(8,128)S(1)}, f32[2,256,256]{2,1,0:T(8,128)}, u32[]{:S(2)}) copy-start(f32[2,256,256]{2,1,0:T(8,128)} %get-tuple-element.21.refs_0_) | copy-start | bytes 1572868
  82.9 0.9 %copy-start.1 = (f32[256,128]{1,0:T(8,128)S(1)}, f32[256,128]{1,0:T(8,128)}, u32[]{:S(2)}) copy-start(f32[256,128]{1,0:T(8,128)} %get-tuple-element.23.refs_2_) | copy-start | bytes 393220
  83.8 0.9 %copy-start.2 = (f32[128,256]{1,0:T(8,128)S(1)}, f32[128,256]{1,0:T(8,128)}, u32[]{:S(2)}) copy-start(f32[128,256]{1,0:T(8,128)} %get-tuple-element.24.refs_3_) | copy-start | bytes 393220
  84.7 0.7 copy-start.3
  85.4 0.6 copy-start.4

commit v2 on v1

v2 whole, which is shorter than its diff:
```python
import types

import jax
import jax.numpy as jnp
from jax import lax
from jax.experimental import pallas as pl
from jax.experimental.pallas import tpu as pltpu
from jax.sharding import PartitionSpec as P

UNROLL = 4
F32 = jnp.float32
BF16 = jnp.bfloat16


def dot(a, b):
    return jnp.dot(a, b, preferred_element_type=F32)


def fold(value):
    return value.reshape(-1, 8, value.shape[1]).sum(axis=0)


def send(source, target, sems, at, peer):
    return pltpu.make_async_remote_copy(
        src_ref=source,
        dst_ref=target,
        send_sem=sems[0].at[at],
        recv_sem=sems[1].at[at],
        device_id=peer,
        device_id_type=pl.DeviceIdType.MESH,
    )


OPERANDS = (
    "init",
    "noise",
    "step",
    "length",
    "obs",
    "seen",
    "w_in",
    "b_in",
    "w_out",
    "b_out",
    "dec",
    "rate",
    "diff",
)
EXCHANGES = ("w_far", "w_near", "b_far")


def fused_kernel(sizes, r):
    rows, width, steps = sizes.rows, sizes.width, sizes.steps
    seen_count, seen_width = sizes.seen_count, sizes.seen_width
    quarters, planes, total = sizes.quarters, sizes.planes, sizes.total
    mine = lax.axis_index("mp")
    batch = lax.axis_index("batch")
    core = lax.rem(batch, 2)
    other = 1 - core
    place = lax.div(batch, 2)
    sibling = (batch + 1 - 2 * core, mine)

    def quarter_at(d):
        return lax.rem(mine + d, quarters)

    def line_peer(d):
        return (batch, quarter_at(d))

    def place_at(d):
        return lax.rem(place + d, planes)

    def plane_peer(d):
        return (2 * place_at(d) + core, mine)

    def arrived(whole, sems):
        send(whole, whole, sems, 0, sibling).wait_recv()

    def departed(whole, sems):
        send(whole, whole, sems, 0, sibling).wait_send()

    far = [2, 1, 3] if quarters == 4 else list(range(1, quarters))

    weights = [
        pltpu.make_async_copy(r.w_in_hbm, r.all_w.at[0, mine], r.load_sem.at[0]),
        pltpu.make_async_copy(r.w_out_hbm, r.all_w.at[1, mine], r.load_sem.at[1]),
        pltpu.make_async_copy(r.b_in_hbm, r.b_own, r.load_sem.at[2]),
    ]
    for copy in weights:
        copy.start()
    loads = []
    for name in OPERANDS:
        if name in ("w_in", "w_out", "b_in"):
            continue
        copy = pltpu.make_async_copy(
            getattr(r, name + "_hbm"), getattr(r, name), r.load_sem.at[3 + len(loads)]
        )
        copy.start()
        loads.append(copy)

    barrier = pltpu.get_barrier_semaphore()
    peers = [sibling] + [line_peer(d) for d in range(1, quarters)]
    peers += [plane_peer(d) for d in range(1, planes)]
    for peer in peers:
        pl.semaphore_signal(barrier, inc=1, device_id=peer, device_id_type=pl.DeviceIdType.MESH)
    for copy in weights:
        copy.wait()
    r.all_b[mine] = jnp.broadcast_to(r.b_own[...].astype(F32)[None, :], (8, width))
    pl.semaphore_wait(barrier, len(peers))

    sent = []
    for d in far:
        own = r.all_w.at[core, mine]
        copy = send(own, own, r.w_far, d - 1, line_peer(d))
        copy.start()
        sent.append(copy)
    for d in far:
        own = r.all_b.at[mine]
        send(own, own, r.b_far, 0, line_peer(d)).start()

    def column(row):
        return jnp.broadcast_to(row, (rows, rows)).T

    for copy in loads:
        copy.wait()
    r.dt[...] = column(r.step[...])
    r.root[...] = jnp.sqrt(r.dt[...])
    r.len[...] = column(r.length[...])
    for j in range(seen_count):
        r.obs_wide[j] = column(r.obs[j : j + 1, :])
    r.target[...] = r.seen[...].astype(F32).reshape(r.target.shape)
    r.pick[...] = jnp.zeros_like(r.pick)
    r.kl[...] = jnp.zeros_like(r.kl)
    r.sum_b_in[...] = jnp.zeros_like(r.sum_b_in)
    r.sum_b_out[...] = jnp.zeros_like(r.sum_b_out)
    r.state[...] = r.init[...]
    r.ones[...] = jnp.ones_like(r.ones)
    dec_t = r.dec[...].T
    r.dec_t[:seen_width, :] = dec_t
    r.dec_t[seen_width:, :] = dec_t

    order = [1, 3, 2] if quarters == 4 else list(range(1, quarters))
    for d in order:
        origin = quarter_at(quarters - d)
        got = r.all_w.at[core, origin]
        send(got, got, r.w_far, d - 1, line_peer(d)).wait_recv()
        send(got, got, r.w_near, 0, sibling).start()
    arrived(r.all_b.at[pl.ds(0, quarters - 1)], r.b_far)
    arrived(r.all_w.at[other, pl.ds(0, quarters - 1)], r.w_near)
    departed(r.all_b.at[pl.ds(0, quarters - 1)], r.b_far)
    departed(r.all_w.at[core, pl.ds(0, quarters - 1)], r.w_near)
    for copy in sent:
        copy.wait_send()

    def both(value):
        return jnp.concatenate([value] * (width // rows), axis=1)

    def look(k, x):
        seen = dot(x, r.dec[...])
        for j in range(seen_count):
            r.pick[j] = jnp.where(r.obs_wide[j] == k, seen, r.pick[j])

    def turn(k, x):
        r.xt[:, pl.ds(pl.multiple_of(k * rows, rows), rows)] = x.T

    def advance(k, state):
        x = state.astype(BF16)
        drift = jnp.broadcast_to(r.b_out[...], (rows, width))
        for n in range(quarters):
            act = jnp.tanh(dot(x, r.all_w[0, n]) + r.all_b[n, :1, :]).astype(BF16)
            r.act[n, pl.ds(k * rows, rows), :] = act
            drift = drift + dot(act, r.all_w[1, n])
        inv = 1.0 / r.diff[...]
        live = k < r.len[...]
        factor = both(jnp.where(live, r.dt[...], 0.0))
        root = both(jnp.where(live, r.root[...], 0.0))
        following = state + (
            factor * drift + r.diff[...] * root * r.noise[k].astype(F32)
        )
        residual = (drift + r.rate[...] * state) * inv
        r.kl[...] += factor * residual * residual
        r.scaled[k] = residual * inv
        turn(k, x)
        look(k, x)
        which = lax.rem(k, 2 * quarters)
        tensor, n = lax.div(which, quarters), lax.rem(which, quarters)
        r.all_t[tensor, n] = r.all_w[tensor, n].T
        return following

    def forward(index, carry):
        state = r.state[...]
        for u in range(sizes.unroll):
            state = advance(index * sizes.unroll + u, state)
        r.state[...] = state
        return carry

    lax.fori_loop(0, steps // sizes.unroll, forward, 0)
    final = r.state[...].astype(BF16)
    look(steps, final)
    turn(steps, final)

    square = jnp.zeros((rows, seen_width), F32)
    for j in range(seen_count):
        misfit = r.pick[j] - r.target[pl.ds(j, rows, stride=seen_count), :]
        square = square + misfit * misfit
        r.pick[j] = misfit.astype(BF16).astype(F32)
    loglik = -0.5 * jnp.sum(square.T, axis=0, keepdims=True)
    kl_half = r.kl[:, :rows]
    for part in range(1, width // rows):
        kl_half = kl_half + r.kl[:, part * rows : (part + 1) * rows]
    kl_row = 0.5 * jnp.sum(kl_half.T, axis=0, keepdims=True)
    divisor = (width * r.length[...] + seen_width * seen_count).astype(F32)
    r.elbo[...] = (loglik - kl_row) / divisor

    def observe(t):
        spread = jnp.zeros((rows, seen_width), F32)
        for j in range(seen_count):
            spread = spread + jnp.where(r.obs_wide[j] == t, r.pick[j], 0.0)
        high = spread.astype(BF16)
        low = (spread - high.astype(F32)).astype(BF16)
        pair = jnp.concatenate([high, low], axis=1)
        r.miss[pl.ds(t * rows, rows), :] = pair
        return dot(pair, r.dec_t[...])

    r.cot[...] = observe(steps)

    def joint(parts):
        half = len(parts) // 2
        first, second = sum(parts[1:half], parts[0]), sum(parts[half + 1 :], parts[half])
        return first * r.ones[...] + second

    def retreat(k, cot):
        scaled = r.scaled[k]
        factor = both(jnp.where(k < r.len[...], r.dt[...], 0.0))
        update = factor * (cot + scaled)
        rounded = update.astype(BF16)
        cot = cot + factor * r.rate[...] * scaled
        cot = cot + observe(k)
        inner = [dot(rounded, r.all_t[1, n]) for n in range(quarters)]
        pres = []
        for n in range(quarters):
            act = r.act[n, pl.ds(k * rows, rows), :].astype(F32)
            pre = inner[n] * (1.0 - act * act)
            pre_round = pre.astype(BF16)
            pres.append(pre_round)
            r.pre[n, pl.ds(k * rows, rows), :] = pre_round
            r.sum_b_in[n] += fold(pre)
        r.ut[:, pl.ds(pl.multiple_of(k * rows, rows), rows)] = rounded.T
        r.sum_b_out[...] += fold(update)
        return cot + joint([dot(pres[n], r.all_t[0, n]) for n in range(quarters)])

    def backward(index, carry):
        cot = r.cot[...]
        for u in range(sizes.unroll):
            cot = retreat(steps - 1 - index * sizes.unroll - u, cot)
        r.cot[...] = cot
        return carry

    lax.fori_loop(0, steps // sizes.unroll, backward, 0)
    for n in range(quarters):
        r.tail[n : n + 1, :] = jnp.sum(r.sum_b_in[n], axis=0, keepdims=True)
    r.tail[quarters : quarters + 1, :] = jnp.sum(r.sum_b_out[...], axis=0, keepdims=True)
    r.tail[quarters + 1 : quarters + 2, :rows] = loglik
    r.tail[quarters + 1 : quarters + 2, rows : 2 * rows] = kl_row
    r.tail[quarters + 2 :, :] = jnp.zeros((r.tail.shape[0] - quarters - 2, width), F32)
    tail_near = send(r.tail, r.tail_sib, r.near, 0, sibling)
    tail_near.start()
    waits = [tail_near]
    leaving = []

    def put(source, target):
        copy = pltpu.make_async_copy(source, target, r.out_sem.at[len(leaving)])
        copy.start()
        leaving.append(copy)

    put(r.elbo, r.elbo_out)
    put(r.cot, r.cot_out)
    dec_grad = dot(r.xt[:, rows:], r.miss[rows:, :])
    dec_grad = dec_grad[:, :seen_width] + dec_grad[:, seen_width:]
    r.dec_part[...] = dec_grad.reshape(r.dec_part.shape)
    dec_near = send(r.dec_part.at[other], r.dec_sib, r.near, 1, sibling)
    dec_near.start()
    waits.append(dec_near)
    dec_rows = r.dec_sum.shape[1]

    def chunk(i, d):
        n = quarter_at(d)
        r.grad[i, 0] = dot(r.xt[:, : steps * rows], r.pre[n])
        r.grad[i, 1] = dot(r.ut[...], r.act[n]).T
        copy = send(r.grad.at[i, other], r.grad_sib.at[i], r.near, 3 + i, sibling)
        copy.start()
        waits.append(copy)
        return copy

    def joined(i, copy):
        copy.wait_recv()
        return r.grad[i, core] + r.grad_sib[i]

    def pass_on(i, d, copy):
        r.line_out[i] = joined(i, copy).astype(BF16)
        send(r.line_out.at[i], r.line_in.at[i], r.line, 0, line_peer(d)).start()

    nears = []
    for i, d in enumerate(far):
        near = chunk(i, d)
        if i == 0:
            tail_near.wait_recv()
            r.tail_sum[...] = r.tail[...] + r.tail_sib[...]
            dec_near.wait_recv()
            r.dec_sum[...] = (r.dec_part[core] + r.dec_sib[...]).reshape(r.dec_sum.shape)
            for e in range(1, planes):
                send(r.tail_sum, r.tail_in.at[e - 1], r.tail_plane, 0, plane_peer(e)).start()
                send(
                    r.dec_sum.at[place_at(e)], r.dec_in.at[e - 1], r.dec_plane, 0, plane_peer(e)
                ).start()
        nears.append(near)
        if i > 0:
            pass_on(i - 1, far[i - 1], nears[i - 1])
    last = len(far)
    near = chunk(last, 0)
    pass_on(last - 1, far[last - 1], nears[last - 1])
    value = r.tail_sum[...]
    arrived(r.tail_in, r.tail_plane)
    for e in range(1, planes):
        value = value + r.tail_in[e - 1]
    r.tail_line[...] = value
    value = r.dec_sum[place]
    arrived(r.dec_in, r.dec_plane)
    for e in range(1, planes):
        value = value + r.dec_in[e - 1]
    r.dec_line[...] = value
    for e in range(1, quarters):
        send(r.tail_line, r.tail_line_in.at[e - 1], r.tail_far, 0, line_peer(e)).start()
        send(r.dec_line, r.dec_line_in.at[e - 1], r.dec_far, 0, line_peer(e)).start()
    value = joined(last, near)
    arrived(r.line_in, r.line)
    for i in range(last):
        value = value + r.line_in[i].astype(F32)
    r.full[...] = value
    r.plane_out[...] = value.astype(BF16).reshape(r.plane_out.shape)
    for e in range(1, planes):
        send(
            r.plane_out.at[place_at(e)], r.plane_in.at[e - 1], r.plane, 0, plane_peer(e)
        ).start()
    piece = width // planes

    def rows_of(tensor, owner):
        return r.res.at[tensor, pl.ds(pl.multiple_of(owner * piece, piece), piece), :]

    value = r.dec_line[...]
    arrived(r.dec_line_in, r.dec_far)
    for e in range(1, quarters):
        value = value + r.dec_line_in[e - 1]
    r.dec_all[core, place] = value / total
    own = r.dec_all.at[core, place]
    for e in range(1, planes):
        send(own, own, r.dec_spread, 0, plane_peer(e)).start()
    value = r.tail_line[...]
    arrived(r.tail_line_in, r.tail_far)
    for e in range(1, quarters):
        value = value + r.tail_line_in[e - 1]
    r.tail_total[...] = value
    scale = 1.0 / total
    r.b_in_sum[...] = r.tail_total[pl.ds(mine, 1), :] * scale
    r.b_out_sum[...] = r.tail_total[quarters : quarters + 1, :] * scale
    points = r.tail_total[quarters + 1 : quarters + 2, :] * scale
    r.scores[:, 0:1] = jnp.sum(points[:, :rows], axis=1, keepdims=True)
    r.scores[:, 1:2] = jnp.sum(points[:, rows : 2 * rows], axis=1, keepdims=True)
    value = r.full[pl.ds(pl.multiple_of(place * piece, piece), piece), :]
    arrived(r.plane_in, r.plane)
    for e in range(1, planes):
        value = value + r.plane_in[e - 1].astype(F32)
    r.res[core, pl.ds(pl.multiple_of(place * piece, piece), piece), :] = value / total
    own = rows_of(core, place)
    for e in range(1, planes):
        send(own, own, r.spread, 0, plane_peer(e)).start()
    arrived(r.dec_all.at[core, pl.ds(0, planes - 1)], r.dec_spread)
    copy = send(r.dec_all.at[core], r.dec_all.at[core], r.near, 2, sibling)
    copy.start()
    waits.append(copy)
    put(r.b_in_sum, r.b_in_out)
    put(r.b_out_sum, r.b_out_out)
    put(r.scores, r.scores_out)
    pieces = pl.ds(0, width - piece)
    arrived(r.res.at[core, pieces], r.spread)
    copy = send(r.res.at[core], r.res.at[core], r.hand, 0, sibling)
    copy.start()
    waits.append(copy)
    got = r.dec_all.at[other]
    send(got, got, r.near, 2, sibling).wait_recv()
    put(r.dec_all, r.dec_out)
    arrived(r.res.at[other], r.hand)
    put(r.res.at[0], r.w_in_out)
    put(r.res.at[1], r.w_out_out)
    departed(r.line_in, r.line)
    departed(r.tail_in, r.tail_plane)
    departed(r.dec_in, r.dec_plane)
    departed(r.tail_line_in, r.tail_far)
    departed(r.dec_line_in, r.dec_far)
    departed(r.dec_all.at[core, pl.ds(0, planes - 1)], r.dec_spread)
    departed(r.plane_in, r.plane)
    departed(r.res.at[core, pieces], r.spread)
    for copy in waits:
        copy.wait_send()
    for copy in leaving:
        copy.wait()


def fused(sizes, operands):
    rows, width, steps = sizes.rows, sizes.width, sizes.steps
    count, seen_width = sizes.seen_count, sizes.seen_width
    quarters, planes = sizes.quarters, sizes.planes
    piece = width // planes
    dec_rows = width // 2 // planes
    outs = {
        "elbo_out": ((1, rows), F32),
        "w_in_out": ((width, width), F32),
        "w_out_out": ((width, width), F32),
        "b_in_out": ((1, width), F32),
        "b_out_out": ((1, width), F32),
        "dec_out": ((2, planes, dec_rows, seen_width), F32),
        "scores_out": ((1, 2), F32),
        "cot_out": ((rows, width), F32),
    }
    arrays = {
        "xt": ((width, (steps + 1) * rows), BF16),
        "ut": ((width, steps * rows), BF16),
        "act": ((quarters, steps * rows, width), BF16),
        "pre": ((quarters, steps * rows, width), BF16),
        "scaled": ((steps, rows, width), F32),
        "pick": ((count, rows, seen_width), F32),
        "obs_wide": ((count, rows, rows), jnp.int32),
        "dt": ((rows, rows), F32),
        "root": ((rows, rows), F32),
        "len": ((rows, rows), jnp.int32),
        "state": ((rows, width), F32),
        "kl": ((rows, width), F32),
        "cot": ((rows, width), F32),
        "ones": ((1, width), F32),
        "sum_b_in": ((quarters, 8, width), F32),
        "sum_b_out": ((8, width), F32),
        "miss": (((steps + 1) * rows, 2 * seen_width), BF16),
        "target": ((rows * count, seen_width), F32),
        "all_w": ((2, quarters, width, width), BF16),
        "all_t": ((2, quarters, width, width), BF16),
        "all_b": ((quarters, 8, width), F32),
        "b_own": (sizes.b_shape, BF16),
        "dec_t": ((2 * seen_width, width), BF16),
        "elbo": ((1, rows), F32),
        "res": ((2, width, width), F32),
        "b_in_sum": ((1, width), F32),
        "b_out_sum": ((1, width), F32),
        "scores": ((1, 2), F32),
        "tail": ((8, width), F32),
        "tail_sib": ((8, width), F32),
        "tail_sum": ((8, width), F32),
        "tail_in": ((planes - 1, 8, width), F32),
        "tail_line": ((8, width), F32),
        "tail_total": ((8, width), F32),
        "tail_line_in": ((quarters - 1, 8, width), F32),
        "dec_part": ((2, width // 2, seen_width), F32),
        "dec_sib": ((width // 2, seen_width), F32),
        "dec_sum": ((planes, dec_rows, seen_width), F32),
        "dec_in": ((planes - 1, dec_rows, seen_width), F32),
        "dec_line": ((dec_rows, seen_width), F32),
        "dec_line_in": ((quarters - 1, dec_rows, seen_width), F32),
        "dec_all": ((2, planes, dec_rows, seen_width), F32),
        "grad": ((quarters, 2, width, width), F32),
        "grad_sib": ((quarters, width, width), F32),
        "line_out": ((quarters - 1, width, width), BF16),
        "line_in": ((quarters - 1, width, width), BF16),
        "full": ((width, width), F32),
        "plane_out": ((planes, piece, width), BF16),
        "plane_in": ((planes - 1, piece, width), BF16),
    }
    for name, value in zip(OPERANDS, operands):
        if name not in ("w_in", "w_out", "b_in"):
            arrays[name] = (value.shape, value.dtype)
    links = {
        "w_far": quarters - 1,
        "w_near": 1,
        "b_far": 1,
        "near": 3 + quarters,
        "line": 1,
        "tail_plane": 1,
        "dec_plane": 1,
        "tail_far": 1,
        "dec_far": 1,
        "dec_spread": 1,
        "plane": 1,
        "spread": 1,
        "hand": 1,
    }
    scratch = [pltpu.VMEM(shape, dtype) for shape, dtype in arrays.values()]
    for number in links.values():
        scratch += [pltpu.SemaphoreType.DMA((number,))] * 2
    scratch.append(pltpu.SemaphoreType.DMA((len(OPERANDS),)))
    scratch.append(pltpu.SemaphoreType.DMA((len(outs),)))

    def body(*refs):
        refs = list(refs)
        r = types.SimpleNamespace()
        for name in OPERANDS:
            setattr(r, name + "_hbm", refs.pop(0))
        for name in list(outs) + list(arrays):
            setattr(r, name, refs.pop(0))
        for name in links:
            setattr(r, name, (refs.pop(0), refs.pop(0)))
        r.load_sem = refs.pop(0)
        r.out_sem = refs.pop(0)
        fused_kernel(sizes, r)

    return pl.pallas_call(
        body,
        out_shape=[jax.ShapeDtypeStruct(shape, dtype) for shape, dtype in outs.values()],
        in_specs=[pl.BlockSpec(memory_space=pltpu.HBM)] * len(OPERANDS),
        out_specs=[pl.BlockSpec(memory_space=pltpu.HBM)] * len(outs),
        scratch_shapes=scratch,
        compiler_params=pltpu.CompilerParams(
            collective_id=0, has_side_effects=True, vmem_limit_bytes=60 * 1024 * 1024
        ),
        name="fused",
    )(*operands)


def finish(arrays):
    number = len(arrays)

    def body(*refs):
        ins, outs, spaces = refs[:number], refs[number : 2 * number], refs[2 * number : 3 * number]
        taken, given = refs[3 * number :]
        loads = [
            pltpu.make_async_copy(source, space, taken.at[i])
            for i, (source, space) in enumerate(zip(ins, spaces))
        ]
        stores = [
            pltpu.make_async_copy(space, target, given.at[i])
            for i, (space, target) in enumerate(zip(spaces, outs))
        ]
        for load in loads:
            load.start()
        for load, store in zip(loads, stores):
            load.wait()
            store.start()
        for store in stores:
            store.wait()

    hbm = pl.BlockSpec(memory_space=pltpu.HBM)
    return pl.pallas_call(
        body,
        out_shape=[jax.ShapeDtypeStruct(value.shape, value.dtype) for value in arrays],
        in_specs=[hbm] * number,
        out_specs=[hbm] * number,
        scratch_shapes=[pltpu.VMEM(value.shape, value.dtype) for value in arrays]
        + [pltpu.SemaphoreType.DMA((number,))] * 2,
        compiler_params=pltpu.CompilerParams(vmem_limit_bytes=60 * 1024 * 1024),
        name="finish",
    )(*arrays)


def on_device(
    init_state,
    brownian,
    step_size,
    lengths,
    obs_steps,
    observed,
    w_in,
    b_in,
    w_out,
    b_out,
    decoder,
    prior_rate,
    diffusion,
):
    rows, width = init_state.shape
    quarters = lax.axis_size("mp")
    members = lax.axis_size("batch")
    sizes = types.SimpleNamespace(
        rows=rows,
        width=width,
        steps=brownian.shape[0],
        seen_count=observed.shape[1],
        seen_width=observed.shape[2],
        quarters=quarters,
        planes=members // 2,
        total=rows * members * quarters,
        unroll=UNROLL,
        b_shape=b_in.shape,
    )
    results = fused(
        sizes,
        (
            init_state,
            brownian,
            step_size[None, :],
            lengths[None, :],
            obs_steps.T,
            observed,
            w_in,
            b_in,
            w_out,
            b_out[None, :],
            decoder,
            prior_rate[None, :],
            diffusion[None, :],
        ),
    )
    elbo, own_w_in, own_w_out, own_b_in, b_out_grad, dec_grad, scores, cot = finish(results)
    dec_grad = dec_grad.reshape(decoder.shape)
    return (
        elbo[0],
        scores[0],
        own_w_in,
        own_b_in[0],
        own_w_out,
        b_out_grad[0],
        dec_grad,
        cot,
    )


def solution(mesh):
    both = ("batch", "mp")
    placed = (
        P(both, None),
        P(None, both, None),
        P(both),
        P(both),
        P(both, None),
        P(both, None, None),
        P(None, "mp"),
        P("mp"),
        P("mp", None),
        P(),
        P(),
        P(),
        P(),
    )
    return jax.shard_map(
        on_device,
        mesh=mesh,
        in_specs=placed,
        out_specs=(
            P(both),
            P(),
            P(None, "mp"),
            P("mp"),
            P("mp", None),
            P(),
            P(),
            P(both, None),
        ),
        check_vma=False,
    )
```

time: 87.2 us -> 71.4 us (0.82)
  Pallas kernels: 80.9 us -> 70.6 us
  local copies, waits for them, and re-layouts: 5.39 us -> 0 us
    pallas_call x1, Pallas kernels: 80 us -> 68.6 us  [fused(): pl.pallas_call(body, out_shape=[jax.ShapeDtypeStruct(shape, dtype) for sh...]
    unnamed x10 -> x0, local copies, waits for them, and re-layouts: 4.17 us -> none
    broadcast_in_dim x1 -> x0, local copies, waits for them, and re-layouts: 1.22 us -> none  [on_device(): b_in[None, :]]
    pallas_call x1, Pallas kernels: 0.91 us -> 1.98 us  [finish(): pl.pallas_call(body, out_shape=[jax.ShapeDtypeStruct(value.shape, value.d...]
where the time goes in v2:
time: 71.4 us; the launch traced here: 71.2 us
  Pallas kernels  70.6 us (99%)
    pallas_call x1, Pallas kernels, fused(): pl.pallas_call(body, out_shape=[jax.ShapeDtypeStruct(shape, dtype) for sh...  68.6 us
    pallas_call x1, Pallas kernels, finish(): pl.pallas_call(body, out_shape=[jax.ShapeDtypeStruct(value.shape, value.d...  1.98 us

profile of v2, /device:TPU:1, one launch (start us, length us, event | category | flops | bytes accessed | tf_op | source)
XLA Modules:
  0.0 71.2 jit_solution(13053389763550197723)
XLA Ops:
  0.6 68.6 %fused.1 = (f32[1,128]{1,0:T(1,128)}, f32[256,256]{1,0:T(8,128)}, f32[256,256]{1,0:T(8,128)}, f32[1,256]{1,0:T(1,128)}, f32[1,256]{1,0:T(1,128)}, /*index=5*/f32...) custom-call(f32[128,256]{1,0:T(8,128)} %refs_0_.1, bf16[32,128,256]{2,1,0:T(8,128)(2,1)} %refs_1_.1, ...), custom_call_target="tpu_custom_call" | custom-call | tf_op jit(solution)/shard_map/fused/pallas_call | solution.py:512
  69.3 2.0 %finish.1 = (f32[1,128]{1,0:T(1,128)}, f32[256,256]{1,0:T(8,128)}, f32[256,256]{1,0:T(8,128)}, f32[1,256]{1,0:T(1,128)}, f32[1,256]{1,0:T(1,128)}, /*index=5*/f3...) custom-call(f32[1,128]{1,0:T(1,128)} %get-tuple-element.24.refs_0_, f32[256,256]{1,0:T(8,128)} %get-tuple-element.25.refs_1_, ...), custom_call_target="tpu_custom_call" | custom-call | tf_op jit(solution)/shard_map/finish/pallas_call | solution.py:548
